TPU v7x, 32 devices: a whole 2x2x4 slice. The times are simulated.
32 devices in a mesh: dp: 2 (over x), expert: 8 (over z, core), tensor: 2 (over y).
Axes of the slice: x: 2, y: 2, z: 4, core: 2. Of those that a mesh axis runs over, the one named last changes fastest.
Arguments:
- tokens: bfloat16 [192, 256, 1280], P(('dp', 'expert', 'tensor')), may hold values from -16 to 16
- cotangent: bfloat16 [192, 256, 1280], P(('dp', 'expert', 'tensor')), may hold values from -6 to 6
- norm_gain: float32 [1280], replicated, may hold values from 0.5 to 1.5
- slot_keys: bfloat16 [1280, 16], replicated, may hold values from -2 to 2
- w_in: bfloat16 [8, 1280, 2560], P('expert', None, 'tensor'), may hold values from -0.15625 to 0.15625
- w_out: bfloat16 [8, 2560, 1280], P('expert', 'tensor'), may hold values from -0.125 to 0.125
Outputs:
- grad_tokens: bfloat16 [192, 256, 1280], P(('dp', 'expert', 'tensor'))
- grad_gain: float32 [1280], replicated
- grad_keys: float32 [1280, 16], replicated
- grad_in: bfloat16 [8, 1280, 2560], P('expert', 'dp', 'tensor')
- grad_out: bfloat16 [8, 2560, 1280], P('expert', 'tensor', 'dp')
All inputs are finite; a program needn't handle non-finite values.
Results may differ from a plain program's by a relative error of at most 0.014.
The roundings to bfloat16 on the way count: a program that leaves them out, or rounds other values in their place, can miss the bound.
Values may be sent and summed in bfloat16 or wider, within the bound.
A program may use at most 128 MiB of HBM per device.

v0:
```python
import jax
import jax.numpy as jnp
from jax import lax
from jax.sharding import PartitionSpec as P

SLOT_PER = 2
EPSILON = 1e-06


def mixing_forward(tokens, gain, slot_keys):
    average = jnp.mean(tokens, axis=-1, keepdims=True, dtype=jnp.float32)
    centred = tokens.astype(jnp.float32) - average
    spread = jnp.mean(centred * centred, axis=-1, keepdims=True)
    inverse = lax.rsqrt(spread + EPSILON)
    scaled = centred * inverse
    normed = (scaled * gain).astype(jnp.bfloat16)
    logits = jnp.einsum("bmd,dn->bmn", normed, slot_keys, preferred_element_type=jnp.float32)
    dispatch = jax.nn.softmax(logits, axis=1)
    combine = jax.nn.softmax(logits, axis=2)
    dispatch_low = dispatch.astype(jnp.bfloat16)
    slot_values = jnp.einsum(
        "bmn,bmd->bnd", dispatch_low, normed, preferred_element_type=jnp.float32
    )
    return (slot_values, combine, (scaled, inverse, normed, dispatch, combine, dispatch_low))


def mixing_backward(saved, gain, slot_keys, slot_grad, combine_grad):
    scaled, inverse, normed, dispatch, combine, dispatch_low = saved
    grad_dispatch = jnp.einsum(
        "bnd,bmd->bmn", slot_grad, normed, preferred_element_type=jnp.float32
    )
    grad_normed = jnp.einsum(
        "bmn,bnd->bmd", dispatch_low, slot_grad, preferred_element_type=jnp.float32
    )
    grad_logits = dispatch * (
        grad_dispatch - jnp.sum(dispatch * grad_dispatch, axis=1, keepdims=True)
    )
    grad_logits = grad_logits + combine * (
        combine_grad - jnp.sum(combine * combine_grad, axis=2, keepdims=True)
    )
    keys_wide = slot_keys.astype(jnp.float32)
    grad_normed = grad_normed + jnp.einsum(
        "bmn,dn->bmd", grad_logits, keys_wide, precision=lax.Precision.HIGHEST
    )
    keys_term = jnp.einsum(
        "bmd,bmn->dn", normed.astype(jnp.float32), grad_logits, precision=lax.Precision.HIGHEST
    )
    gain_term = jnp.sum(grad_normed * scaled, axis=(0, 1))
    grad_scaled = grad_normed * gain
    first_mean = jnp.mean(grad_scaled, axis=-1, keepdims=True)
    second_mean = jnp.mean(grad_scaled * scaled, axis=-1, keepdims=True)
    grad_tok = inverse * (grad_scaled - first_mean - scaled * second_mean)
    return (grad_tok, gain_term, keys_term)


def contract_rows(left, right):
    return lax.dot_general(
        left, right, (((0,), (0,)), ((), ())), preferred_element_type=jnp.float32
    )


def contract_cols(left, right):
    return lax.dot_general(
        left, right, (((1,), (1,)), ((), ())), preferred_element_type=jnp.float32
    )


def local(tokens, cotangent, norm_gain, slot_keys, w_in, w_out):
    local_imgs, token_count, features = tokens.shape
    slot_count = slot_keys.shape[1]
    experts = slot_count // SLOT_PER
    slot_values, combine, saved = mixing_forward(tokens, norm_gain, slot_keys)
    slot_inputs = slot_values.astype(jnp.bfloat16).reshape(local_imgs, experts, SLOT_PER, features)
    arrived = lax.all_to_all(slot_inputs, "expert", split_axis=1, concat_axis=0, tiled=True)
    slot_rows = lax.all_gather(arrived, "tensor", axis=0, tiled=True).reshape(-1, features)
    first_proj = w_in[0]
    second_proj = w_out[0]
    pre_act = jnp.dot(slot_rows, first_proj, preferred_element_type=jnp.float32)
    hidden = jax.nn.gelu(pre_act).astype(jnp.bfloat16)
    segment = hidden
    outputs = lax.psum_scatter(
        jnp.dot(segment, second_proj, preferred_element_type=jnp.float32),
        "tensor",
        scatter_dimension=0,
        tiled=True,
    )
    outputs = outputs.astype(jnp.bfloat16).reshape(arrived.shape)
    returned = lax.all_to_all(outputs, "expert", split_axis=0, concat_axis=1, tiled=True).reshape(
        local_imgs, slot_count, features
    )
    combine_low = combine.astype(jnp.bfloat16)
    grad_slots = jnp.einsum(
        "bmn,bmd->bnd", combine_low, cotangent, preferred_element_type=jnp.float32
    )
    grad_slots = grad_slots.astype(jnp.bfloat16).reshape(local_imgs, experts, SLOT_PER, features)
    grad_combine = jnp.einsum(
        "bmd,bnd->bmn", cotangent, returned, preferred_element_type=jnp.float32
    )
    grads_sent = lax.all_to_all(grad_slots, "expert", split_axis=1, concat_axis=0, tiled=True)
    grad_rows = lax.all_gather(grads_sent, "tensor", axis=0, tiled=True).reshape(-1, features)
    grad_hidden = contract_cols(grad_rows, second_proj)
    grad_pre = jax.vjp(jax.nn.gelu, pre_act)[1](grad_hidden)[0].astype(jnp.bfloat16)
    segment = grad_pre
    grad_in_rows = lax.psum_scatter(
        contract_cols(segment, first_proj), "tensor", scatter_dimension=0, tiled=True
    )
    grad_in_rows = grad_in_rows.astype(jnp.bfloat16).reshape(arrived.shape)
    grad_back = lax.all_to_all(
        grad_in_rows, "expert", split_axis=0, concat_axis=1, tiled=True
    ).reshape(local_imgs, slot_count, features)
    grad_tok, gain_term, keys_term = mixing_backward(
        saved, norm_gain, slot_keys, grad_back, grad_combine
    )
    grad_tokens = (cotangent.astype(jnp.float32) + grad_tok).astype(jnp.bfloat16)
    grad_gain, grad_keys = lax.psum((gain_term, keys_term), ("dp", "expert", "tensor"))
    split_rows, split_grads = (
        lax.all_to_all(slot_rows, "dp", split_axis=1, concat_axis=0, tiled=True),
        lax.all_to_all(grad_rows, "dp", split_axis=1, concat_axis=0, tiled=True),
    )
    first_total = contract_rows(split_rows, lax.all_gather(grad_pre, "dp", axis=0, tiled=True))
    second_total = contract_rows(lax.all_gather(hidden, "dp", axis=0, tiled=True), split_grads)
    return (
        grad_tokens,
        grad_gain,
        grad_keys,
        first_total.astype(jnp.bfloat16)[None],
        second_total.astype(jnp.bfloat16)[None],
    )


def solution(mesh):
    placed = (
        P(("dp", "expert", "tensor"), None, None),
        P(("dp", "expert", "tensor"), None, None),
        P(),
        P(),
        P("expert", None, "tensor"),
        P("expert", "tensor", None),
    )
    return jax.shard_map(
        local,
        mesh=mesh,
        in_specs=placed,
        out_specs=(
            P(("dp", "expert", "tensor"), None, None),
            P(),
            P(),
            P("expert", "dp", "tensor"),
            P("expert", "tensor", "dp"),
        ),
        check_vma=False,
    )
```

profile of v0, /device:TPU:8, one launch (start us, length us, event | category | flops | bytes accessed | tf_op | source)
XLA Modules:
  0.0 315.5 jit_solution(6597556359371723776)
XLA Ops:
  7.2 2.8 convert_reduce_fusion
  10.1 3.4 %fusion.15 = f32[6,256]{1,0:T(8,128)S(1)} fusion(bf16[6,256,1280]{2,1,0:T(8,128)(2,1)} %param.6, f32[6,256]{1,0:T(8,128)S(1)} %broadcast_multiply_fusion.2), kind=kLoop, calls=%fused_computation.17 | loop fusion | flops 7862784 | bytes 3944448 | tf_op jit(solution)/shard_map/reduce_sum | solution.py:13
  13.5 1.6 fusion.41
  15.9 4.2 %convolution_convert_fusion.2 = bf16[6,16,1280]{2,1,0:T(8,128)(2,1)} fusion(f32[6,16]{1,0:T(8,128)S(1)} %get-tuple-element.8, f32[6,256,16]{1,2,0:T(8,128)S(1)} %fusion.41, bf16[6,256,1280]{2,1,0:T(8,128)(2,1)} %param.6, f32[1280]{0:T(1024)S(1)} %copy-done.6, f32[6,256]{1,0:T(8,128)S(1)} %add_rsqrt_fusion, f32[6,256]{1,0:T(8,128)S(1)} %broadcast_multiply_fusion.2), kind=kOutput, calls=%fused_computation.32 | convolution fusion | flops 72941920 | bytes 4294016 | tf_op jit(solution)/shard_map/bmn,bmd->bnd/dot_general | solution.py:21
  20.1 1.0 reshape.73
  21.1 0.9 copy.39
  22.0 5.3 %all-to-all-start.1 = ((bf16[6,8,2,1280]{3,2,0,1:T(2,128)(2,1)}), bf16[6,8,2,1280]{3,2,0,1:T(2,128)(2,1)S(1)}, u32[]{:S(2)}, u32[]{:S(2)}) async-start(bf16[6,8,2,1280]{3,2,0,1:T(2,128)(2,1)} %copy.39), calls=%async_computation.1 | async-start | bytes 491520 | tf_op jit(solution)/shard_map/all_to_all | solution.py:74
  27.3 1.6 fusion.52
  28.9 3.5 %convolution_convert_fusion.3 = bf16[6,16,1280]{2,1,0:T(8,128)(2,1)} fusion(bf16[6,256,1280]{2,1,0:T(8,128)(2,1)} %param.7, f32[6,256]{1,0:T(8,128)S(1)} %get-tuple-element.10, f32[6,256,16]{1,2,0:T(8,128)} %copy-done.3), kind=kOutput, calls=%fused_computation.33 | convolution fusion | flops 63112720 | bytes 4282368 | tf_op jit(solution)/shard_map/bmn,bmd->bnd/dot_general | solution.py:92
  32.5 1.7 reshape.71
  34.2 1.8 copy.37
  36.0 5.1 %all-to-all-start = ((bf16[6,8,2,1280]{3,2,0,1:T(2,128)(2,1)}), bf16[6,8,2,1280]{3,2,0,1:T(2,128)(2,1)}, u32[]{:S(2)}, u32[]{:S(2)}) async-start(bf16[6,8,2,1280]{3,2,0,1:T(2,128)(2,1)} %copy.37), calls=%async_computation | async-start | bytes 491520 | tf_op jit(solution)/shard_map/all_to_all | solution.py:99
  41.1 8.7 %all_gather.13 = bf16[96,1,2,1280]{3,2,1,0:T(2,128)(2,1)} all-gather(bf16[48,1,2,1280]{3,2,1,0:T(2,128)(2,1)S(1)} %bitcast.84), channel_id=1, replica_groups=mesh['dp'=2,'expert'=8,'tensor'=2] {'tensor'}, dimensions={0}, use_global_device_ids=true | all-gather | bytes 737280 | tf_op jit(solution)/shard_map/all_gather | solution.py:75
  49.9 2.0 reshape.74
  51.9 10.7 %all_gather.12 = bf16[96,1,2,1280]{3,2,1,0:T(2,128)(2,1)} all-gather(bf16[48,1,2,1280]{3,2,1,0:T(2,128)(2,1)} %bitcast.4), channel_id=1, replica_groups=mesh['dp'=2,'expert'=8,'tensor'=2] {'tensor'}, dimensions={0}, use_global_device_ids=true | all-gather | bytes 737280 | tf_op jit(solution)/shard_map/all_gather | solution.py:100
  62.6 2.0 reshape.72
  64.6 2.7 multiply_convert_fusion
  67.3 3.5 %fusion.36 = bf16[192,1280]{1,0:T(8,128)(2,1)S(1)} fusion(f32[192,1280]{1,0:T(8,128)S(1)} %get-tuple-element.13, bf16[192,1280]{1,0:T(8,128)(2,1)} %reshape.72, bf16[1,1280,1280]{2,1,0:T(8,128)(2,1)} %param.11), kind=kOutput, calls=%fused_computation.48 | convolution fusion | flops 634060800 | bytes 5242880 | tf_op jit(solution)/shard_map/dot_general | solution.py:63
  71.6 2.2 fusion.16
  73.8 3.8 %fusion.20 = f32[192,1280]{1,0:T(8,128)} fusion(bf16[192,1280]{1,0:T(8,128)(2,1)} %get-tuple-element.12, bf16[1,1280,1280]{2,1,0:T(8,128)(2,1)} %param.11), kind=kOutput, calls=%fused_computation.24 | convolution fusion | flops 629145600 | bytes 4751360 | tf_op jit(solution)/shard_map/dot_general | solution.py:82
  77.7 2.1 all_to_all.90
  79.8 2.2 all_to_all.94
  82.0 1.9 copy.45
  83.9 4.2 %all-to-all-start.4 = ((bf16[192,2,640]{2,0,1:T(8,128)(2,1)}), bf16[192,2,640]{2,0,1:T(8,128)(2,1)}, u32[]{:S(2)}, u32[]{:S(2)}) async-start(bf16[192,2,640]{2,0,1:T(8,128)(2,1)} %copy.45), calls=%async_computation.6 | async-start | bytes 983040 | tf_op jit(solution)/shard_map/all_to_all | solution.py:117
  88.1 1.9 copy.46
  90.0 15.4 %all_gather.14 = bf16[384,1280]{1,0:T(8,128)(2,1)} all-gather(bf16[192,1280]{1,0:T(8,128)(2,1)} %copy-done.2), channel_id=1, replica_groups=mesh['dp'=2,'expert'=8,'tensor'=2] {'dp'}, dimensions={0}, use_global_device_ids=true | all-gather | bytes 1474560 | tf_op jit(solution)/shard_map/all_gather | solution.py:120
  105.4 4.2 %all-to-all-start.5 = ((bf16[192,2,640]{2,0,1:T(8,128)(2,1)}), bf16[192,2,640]{2,0,1:T(8,128)(2,1)}, u32[]{:S(2)}, u32[]{:S(2)}) async-start(bf16[192,2,640]{2,0,1:T(8,128)(2,1)} %copy.46), calls=%async_computation.7 | async-start | bytes 983040 | tf_op jit(solution)/shard_map/all_to_all | solution.py:118
  109.6 17.4 %all_gather.15 = bf16[384,1280]{1,0:T(8,128)(2,1)} all-gather(bf16[192,1280]{1,0:T(8,128)(2,1)} %get-tuple-element.12), channel_id=1, replica_groups=mesh['dp'=2,'expert'=8,'tensor'=2] {'dp'}, dimensions={0}, use_global_device_ids=true | all-gather | bytes 1474560 | tf_op jit(solution)/shard_map/all_gather | solution.py:121
  127.0 1.1 convert_element_type.53
  128.9 5.1 %all-to-all-start.2 = ((bf16[48,1,2,1280]{3,2,1,0:T(2,128)(2,1)}), bf16[48,1,2,1280]{3,2,1,0:T(2,128)(2,1)S(1)}, u32[]{:S(2)}, u32[]{:S(2)}) async-start(bf16[48,1,2,1280]{3,2,1,0:T(2,128)(2,1)} %bitcast.85), calls=%async_computation.3 | async-start | bytes 491520 | tf_op jit(solution)/shard_map/all_to_all | solution.py:108
  133.9 3.6 %fusion.24 = bf16[1,640,1280]{2,1,0:T(8,128)(2,1)} fusion(bf16[384,640]{1,0:T(8,128)(2,1)} %bitcast.20, bf16[384,1280]{1,0:T(8,128)(2,1)} %all_gather.14), kind=kOutput, calls=%fused_computation.30 | convolution fusion | flops 629964800 | bytes 3112960 | tf_op jit(solution)/shard_map/dot_general | solution.py:57
  137.5 3.6 %fusion.25 = bf16[1,1280,640]{2,1,0:T(8,128)(2,1)} fusion(bf16[384,1280]{1,0:T(8,128)(2,1)} %all_gather.15, bf16[384,640]{1,0:T(8,128)(2,1)} %bitcast.23), kind=kOutput, calls=%fused_computation.31 | convolution fusion | flops 629964800 | bytes 3112960 | tf_op jit(solution)/shard_map/dot_general | solution.py:57
  141.2 1.7 convert_element_type.55
  142.9 1.7 reshape.77
  144.6 5.1 %all-to-all-start.3 = ((bf16[48,1,2,1280]{3,2,1,0:T(2,128)(2,1)}), bf16[48,1,2,1280]{3,2,1,0:T(2,128)(2,1)}, u32[]{:S(2)}, u32[]{:S(2)}) async-start(bf16[48,1,2,1280]{3,2,1,0:T(2,128)(2,1)} %bitcast.86), calls=%async_computation.5 | async-start | bytes 491520 | tf_op jit(solution)/shard_map/all_to_all | solution.py:88
  150.6 1.0 reshape.76
  151.7 4.1 %multiply_reduce_fusion.2 = (f32[6,16]{1,0:T(8,128)S(1)}, f32[6,256,16]{1,2,0:T(8,128)}) fusion(f32[6,256,16]{1,2,0:T(8,128)} %get-tuple-element.9, f32[6,16]{1,0:T(8,128)S(1)} %get-tuple-element.8, bf16[6,16,1280]{2,1,0:T(8,128)(2,1)S(1)} %reshape.76, bf16[6,256,1280]{2,1,0:T(8,128)(2,1)} %param.6, f32[1280]{0:T(1024)} %param.8, ...), kind=kOutput, calls=%fused_computation.54 | convolution fusion | flops 72818592 | bytes 4392704 | tf_op jit(solution)/shard_map/bnd,bmd->bmn/dot_general | solution.py:29
  155.8 5.4 %fusion.43 = f32[6,256,1280]{2,1,0:T(8,128)} fusion(bf16[6,16,1280]{2,1,0:T(8,128)(2,1)S(1)} %reshape.76, f32[6,16]{1,0:T(8,128)S(1)} %get-tuple-element.8, f32[6,256,16]{1,2,0:T(8,128)} %copy-done.3), kind=kOutput, calls=%fused_computation.61 | convolution fusion | flops 62988640 | bytes 8208768 | tf_op jit(solution)/shard_map/bmn,bnd->bmd/dot_general | solution.py:32
  161.1 1.8 copy.49
  162.9 1.0 reshape.78
  164.0 3.3 %multiply_reduce_fusion.1 = (f32[6,256]{1,0:T(8,128)S(1)}, f32[6,256,16]{1,2,0:T(8,128)S(1)}) fusion(f32[6,256,16]{1,2,0:T(8,128)} %get-tuple-element.11, f32[6,256]{1,0:T(8,128)S(1)} %get-tuple-element.10, bf16[6,16,1280]{2,1,0:T(8,128)(2,1)S(1)} %reshape.78, bf16[6,256,1280]{2,1,0:T(8,128)(2,1)} %param.7), kind=kOutput, calls=%fused_computation.53 | convolution fusion | flops 62986752 | bytes 4386816 | tf_op jit(solution)/shard_map/bmd,bnd->bmn/dot_general | solution.py:96
  167.3 1.1 multiply_add_fusion
  168.4 4.5 %convolution_bitcast_fusion = f32[1280,16]{0,1:T(8,128)} fusion(f32[6,256,16]{1,2,0:T(8,128)S(1)} %multiply_add_fusion, bf16[6,256,1280]{2,1,0:T(8,128)(2,1)} %param.6, f32[1280]{0:T(1024)} %param.8, f32[6,256]{1,0:T(8,128)S(1)} %add_rsqrt_fusion, f32[6,256]{1,0:T(8,128)S(1)} %broadcast_multiply_fusion.2), kind=kOutput, calls=%fused_computation.34 | convolution fusion | flops 387317760 | bytes 4129792 | tf_op jit(solution)/shard_map/bmd,bmn->dn/dot_general | solution.py:45
  172.9 10.6 %fusion.14 = (f32[1280]{0:T(1024)S(1)}, f32[6,256]{1,0:T(8,128)S(1)}, f32[6,256]{1,0:T(8,128)S(1)}, f32[6,256,1280]{2,1,0:T(8,128)}) fusion(bf16[6,256,1280]{2,1,0:T(8,128)(2,1)} %param.6, f32[6,256]{1,0:T(8,128)S(1)} %add_rsqrt_fusion, f32[6,256]{1,0:T(8,128)S(1)} %broadcast_multiply_fusion.2, f32[1280]{0:T(1024)S(1)} %copy-done.7, ...), kind=kOutput, calls=%fused_computation.16 | convolution fusion | flops 397143808 | bytes 19834880 | tf_op jit(solution)/shard_map/bmn,dn->bmd/dot_general | solution.py:42
  183.5 8.4 %fusion.13 = bf16[6,256,1280]{2,1,0:T(8,128)(2,1)} fusion(bf16[6,256,1280]{2,1,0:T(8,128)(2,1)} %param.6, bf16[6,256,1280]{2,1,0:T(8,128)(2,1)} %param.7, f32[6,256,1280]{2,1,0:T(8,128)} %get-tuple-element.18, f32[6,256]{1,0:T(8,128)S(1)} %get-tuple-element.19, f32[6,256]{1,0:T(8,128)S(1)} %get-tuple-element.20, f32[1280]{0:T(1024)S(1)} %copy-done.7, ...), kind=kLoop, calls=%fused_computation.15 | loop fusion | flops 21626880 | bytes 19690496 | tf_op jit(solution)/shard_map/convert_element_type | solution.py:114
  191.9 39.3 %psum.14 = f32[1280]{0:T(1024)} all-reduce(f32[1280]{0:T(1024)S(1)} %get-tuple-element.5), channel_id=1, replica_groups=mesh['dp'=2,'expert'=8,'tensor'=2] {'dp','expert','tensor'}, use_global_device_ids=true, to_apply=%region_13.0 | all-reduce | flops 1280 | bytes 10240 | tf_op jit(solution)/shard_map/psum | solution.py:115
  231.2 76.2 %all-reduce.2.cloned.1.call-done = f32[1280,16]{0,1:T(8,128)} async-done(((f32[1280,16]{0,1:T(8,128)}), f32[1280,16]{0,1:T(8,128)}) %all-reduce.2.cloned.1.call-update) | async-done | bytes 81936 | tf_op jit(solution)/shard_map/psum | solution.py:115
  307.4 1.5 copy.52
  (36 shorter events, 3.4 us)
Async XLA Ops:
  7.2 57.4 %copy-start = (bf16[1,1280,1280]{2,1,0:T(8,128)(2,1)S(1)}, bf16[1,1280,1280]{2,1,0:T(8,128)(2,1)}, u32[]{:S(2)}) copy-start(bf16[1,1280,1280]{2,1,0:T(8,128)(2,1)} %param.10) | copy-start | bytes 9830404
  7.2 6.3 %copy-start.1 = (bf16[6,256,1280]{2,1,0:T(8,128)(2,1)S(1)}, bf16[6,256,1280]{2,1,0:T(8,128)(2,1)}, u32[]{:S(2)}) copy-start(bf16[6,256,1280]{2,1,0:T(8,128)(2,1)} %param.6) | copy-start | bytes 11796484
  7.2 6.3 %copy-start.6 = (f32[1280]{0:T(1024)S(1)}, f32[1280]{0:T(1024)}, u32[]{:S(2)}) copy-start(f32[1280]{0:T(1024)} %param.8) | copy-start | bytes 15364
  7.2 6.3 %copy-start.4 = (bf16[1280,16]{0,1:T(8,128)(2,1)S(1)}, bf16[1280,16]{0,1:T(8,128)(2,1)}, u32[]{:S(2)}) copy-start(bf16[1280,16]{0,1:T(8,128)(2,1)} %param.9) | copy-start | bytes 122884
  15.1 0.8 copy-start.3
  22.0 14.0 %all-to-all-start.1 = ((bf16[6,8,2,1280]{3,2,0,1:T(2,128)(2,1)}), bf16[6,8,2,1280]{3,2,0,1:T(2,128)(2,1)S(1)}, u32[]{:S(2)}, u32[]{:S(2)}) async-start(bf16[6,8,2,1280]{3,2,0,1:T(2,128)(2,1)} %copy.39), calls=%async_computation.1 | async-start | bytes 491520 | tf_op jit(solution)/shard_map/all_to_all | solution.py:74
  36.0 15.8 %all-to-all-start = ((bf16[6,8,2,1280]{3,2,0,1:T(2,128)(2,1)}), bf16[6,8,2,1280]{3,2,0,1:T(2,128)(2,1)}, u32[]{:S(2)}, u32[]{:S(2)}) async-start(bf16[6,8,2,1280]{3,2,0,1:T(2,128)(2,1)} %copy.37), calls=%async_computation | async-start | bytes 491520 | tf_op jit(solution)/shard_map/all_to_all | solution.py:99
  41.1 85.9 %reduce-scatter.3.cloned.1.call-start = ((), (), s32[]{:S(2)}) async-start(), calls=%async_computation.8 | async-start | bytes 1474560 | tf_op jit(solution)/shard_map/reduce_scatter | solution.py:104
  70.8 0.8 copy-start.2
  73.8 67.4 %reduce-scatter.5.cloned.1.call-start = ((), (), s32[]{:S(2)}) async-start(), calls=%async_computation.9 | async-start | bytes 1474560 | tf_op jit(solution)/shard_map/reduce_scatter | solution.py:81
  83.9 21.5 %all-to-all-start.4 = ((bf16[192,2,640]{2,0,1:T(8,128)(2,1)}), bf16[192,2,640]{2,0,1:T(8,128)(2,1)}, u32[]{:S(2)}, u32[]{:S(2)}) async-start(bf16[192,2,640]{2,0,1:T(8,128)(2,1)} %copy.45), calls=%async_computation.6 | async-start | bytes 983040 | tf_op jit(solution)/shard_map/all_to_all | solution.py:117
  105.4 23.5 %all-to-all-start.5 = ((bf16[192,2,640]{2,0,1:T(8,128)(2,1)}), bf16[192,2,640]{2,0,1:T(8,128)(2,1)}, u32[]{:S(2)}, u32[]{:S(2)}) async-start(bf16[192,2,640]{2,0,1:T(8,128)(2,1)} %copy.46), calls=%async_computation.7 | async-start | bytes 983040 | tf_op jit(solution)/shard_map/all_to_all | solution.py:118
  128.9 15.8 %all-to-all-start.2 = ((bf16[48,1,2,1280]{3,2,1,0:T(2,128)(2,1)}), bf16[48,1,2,1280]{3,2,1,0:T(2,128)(2,1)S(1)}, u32[]{:S(2)}, u32[]{:S(2)}) async-start(bf16[48,1,2,1280]{3,2,1,0:T(2,128)(2,1)} %bitcast.85), calls=%async_computation.3 | async-start | bytes 491520 | tf_op jit(solution)/shard_map/all_to_all | solution.py:108
  144.6 16.5 %all-to-all-start.3 = ((bf16[48,1,2,1280]{3,2,1,0:T(2,128)(2,1)}), bf16[48,1,2,1280]{3,2,1,0:T(2,128)(2,1)}, u32[]{:S(2)}, u32[]{:S(2)}) async-start(bf16[48,1,2,1280]{3,2,1,0:T(2,128)(2,1)} %bitcast.86), calls=%async_computation.5 | async-start | bytes 491520 | tf_op jit(solution)/shard_map/all_to_all | solution.py:88
  149.7 157.7 %all-reduce.2.cloned.1.call-start = ((), (), s32[]{:S(2)}) async-start(), calls=%async_computation.10 | async-start | bytes 163840 | tf_op jit(solution)/shard_map/psum | solution.py:115
  167.3 5.6 %copy-start.5 = (bf16[1280,16]{0,1:T(8,128)(2,1)S(1)}, bf16[1280,16]{0,1:T(8,128)(2,1)}, u32[]{:S(2)}) copy-start(bf16[1280,16]{0,1:T(8,128)(2,1)} %param.9) | copy-start | bytes 122884
  167.3 5.6 %copy-start.7 = (f32[1280]{0:T(1024)S(1)}, f32[1280]{0:T(1024)}, u32[]{:S(2)}) copy-start(f32[1280]{0:T(1024)} %param.8) | copy-start | bytes 15364
Sparse Core Ops, SparseCore 0:
  73.9 19.6 reduce-scatter.2
  96.4 19.6 reduce-scatter.4
  183.6 123.7 all-reduce.1
where the time goes:
time: 317 us; the launch traced here: 316 us
  blocking collectives  91.5 us (29%)
  waiting for transfers between devices  76.3 us (24%)
  matrix products  56.6 us (18%)
  starting transfers between devices  29.1 us (9%)
  local copies, waits for them, and re-layouts  27.1 us (9%)
  other arithmetic  21 us (7%)
  between operations  13.9 us (4%)
    psum x1, waiting for transfers between devices, local(): lax.psum((gain_term, keys_term), ('dp', 'expert', 'tensor'))  76.2 us
    psum x1, blocking collectives, local(): lax.psum((gain_term, keys_term), ('dp', 'expert', 'tensor'))  39.3 us
    all_gather x1, blocking collectives, local(): lax.all_gather(hidden, 'dp', axis=0, tiled=True)  17.4 us
    all_gather x1, blocking collectives, local(): lax.all_gather(grad_pre, 'dp', axis=0, tiled=True)  15.4 us
    all_gather x1, blocking collectives, local(): lax.all_gather(grads_sent, 'tensor', axis=0, tiled=True)  10.7 us
    dot_general x1, matrix products, mixing_backward(): jnp.einsum('bmn,dn->bmd', grad_logits, keys_wide, precision=lax.Precision...  10.6 us
    all_gather x1, blocking collectives, local(): lax.all_gather(arrived, 'tensor', axis=0, tiled=True).reshape(-1, features)  8.73 us
    convert_element_type x1, other arithmetic, local(): (cotangent.astype(jnp.float32) + grad_tok).astype(jnp.bfloat16)  8.39 us
  transfers between devices with their start and end apart: 9, of which 1 were waited for; matrix products, arithmetic and copies ran while one was open for 16% of the time, Pallas kernels for 0%

commit v1 on v0

--- a/solution.py
+++ b/solution.py
@@ -5,6 +5,11 @@
 
 SLOT_PER = 2
 EPSILON = 1e-06
+
+
+def by_each_axis(value, inner_axis, outer_axis):
+    inner = lax.psum(value, inner_axis)
+    return lax.psum(inner, outer_axis)
 
 
 def mixing_forward(tokens, gain, slot_keys):
@@ -112,7 +117,7 @@
         saved, norm_gain, slot_keys, grad_back, grad_combine
     )
     grad_tokens = (cotangent.astype(jnp.float32) + grad_tok).astype(jnp.bfloat16)
-    grad_gain, grad_keys = lax.psum((gain_term, keys_term), ("dp", "expert", "tensor"))
+    grad_gain, grad_keys = by_each_axis((gain_term, keys_term), ("expert", "tensor"), "dp")
     split_rows, split_grads = (
         lax.all_to_all(slot_rows, "dp", split_axis=1, concat_axis=0, tiled=True),
         lax.all_to_all(grad_rows, "dp", split_axis=1, concat_axis=0, tiled=True),

time: 317 us -> 328 us (1.035)
  the two profiles are of different devices: /device:TPU:8 before, /device:TPU:0 now
where the time goes in v1:
time: 328 us; the launch traced here: 326 us
  blocking collectives  92.3 us (28%)
  waiting for transfers between devices  87.4 us (27%)
  matrix products  56.6 us (17%)
  starting transfers between devices  28 us (9%)
  local copies, waits for them, and re-layouts  27 us (8%)
  other arithmetic  21 us (6%)
  between operations  14 us (4%)
    psum x1, waiting for transfers between devices, by_each_axis(): inner = lax.psum(value, inner_axis)  86.7 us
    psum x1, blocking collectives, by_each_axis(): inner = lax.psum(value, inner_axis)  32.9 us
    all_gather x1, blocking collectives, local(): lax.all_gather(hidden, 'dp', axis=0, tiled=True)  17.8 us
    all_gather x1, blocking collectives, local(): lax.all_gather(grad_pre, 'dp', axis=0, tiled=True)  15.8 us
    all_gather x1, blocking collectives, local(): lax.all_gather(grads_sent, 'tensor', axis=0, tiled=True)  11.1 us
    dot_general x1, matrix products, mixing_backward(): jnp.einsum('bmn,dn->bmd', grad_logits, keys_wide, precision=lax.Precision...  10.6 us
    all_gather x1, blocking collectives, local(): lax.all_gather(arrived, 'tensor', axis=0, tiled=True).reshape(-1, features)  9.08 us
    convert_element_type x1, other arithmetic, local(): (cotangent.astype(jnp.float32) + grad_tok).astype(jnp.bfloat16)  8.38 us
  transfers between devices with their start and end apart: 10, of which 2 were waited for; matrix products, arithmetic and copies ran while one was open for 16% of the time, Pallas kernels for 0%

profile of v1, /device:TPU:0, one launch (start us, length us, event | category | flops | bytes accessed | tf_op | source)
XLA Modules:
  0.0 326.3 jit_solution(10600549730287297328)
XLA Ops:
  7.2 2.8 convert_reduce_fusion
  10.1 3.4 %fusion.15 = f32[6,256]{1,0:T(8,128)S(1)} fusion(bf16[6,256,1280]{2,1,0:T(8,128)(2,1)} %param.6, f32[6,256]{1,0:T(8,128)S(1)} %broadcast_multiply_fusion.2), kind=kLoop, calls=%fused_computation.17 | loop fusion | flops 7862784 | bytes 3944448 | tf_op jit(solution)/shard_map/reduce_sum | solution.py:18
  13.5 1.6 fusion.41
  15.9 4.2 %convolution_convert_fusion.2 = bf16[6,16,1280]{2,1,0:T(8,128)(2,1)} fusion(f32[6,16]{1,0:T(8,128)S(1)} %get-tuple-element.8, f32[6,256,16]{1,2,0:T(8,128)S(1)} %fusion.41, bf16[6,256,1280]{2,1,0:T(8,128)(2,1)} %param.6, f32[1280]{0:T(1024)S(1)} %copy-done.6, f32[6,256]{1,0:T(8,128)S(1)} %add_rsqrt_fusion, f32[6,256]{1,0:T(8,128)S(1)} %broadcast_multiply_fusion.2), kind=kOutput, calls=%fused_computation.32 | convolution fusion | flops 72941920 | bytes 4294016 | tf_op jit(solution)/shard_map/bmn,bmd->bnd/dot_general | solution.py:26
  20.1 1.0 reshape.73
  22.0 6.4 %all-to-all-start.1 = ((bf16[6,8,2,1280]{3,2,0,1:T(2,128)(2,1)}), bf16[6,8,2,1280]{3,2,0,1:T(2,128)(2,1)S(1)}, u32[]{:S(2)}, u32[]{:S(2)}) async-start(bf16[6,8,2,1280]{3,2,0,1:T(2,128)(2,1)} %copy.39), calls=%async_computation.1 | async-start | bytes 491520 | tf_op jit(solution)/shard_map/all_to_all | solution.py:79
  28.3 1.6 fusion.52
  30.0 3.5 %convolution_convert_fusion.3 = bf16[6,16,1280]{2,1,0:T(8,128)(2,1)} fusion(bf16[6,256,1280]{2,1,0:T(8,128)(2,1)} %param.7, f32[6,256]{1,0:T(8,128)S(1)} %get-tuple-element.10, f32[6,256,16]{1,2,0:T(8,128)} %copy-done.3), kind=kOutput, calls=%fused_computation.33 | convolution fusion | flops 63112720 | bytes 4282368 | tf_op jit(solution)/shard_map/bmn,bmd->bnd/dot_general | solution.py:97
  33.5 1.7 reshape.71
  35.2 1.8 copy.37
  37.7 4.5 %all-to-all-start = ((bf16[6,8,2,1280]{3,2,0,1:T(2,128)(2,1)}), bf16[6,8,2,1280]{3,2,0,1:T(2,128)(2,1)}, u32[]{:S(2)}, u32[]{:S(2)}) async-start(bf16[6,8,2,1280]{3,2,0,1:T(2,128)(2,1)} %copy.37), calls=%async_computation | async-start | bytes 491520 | tf_op jit(solution)/shard_map/all_to_all | solution.py:104
  42.2 9.1 %all_gather.13 = bf16[96,1,2,1280]{3,2,1,0:T(2,128)(2,1)} all-gather(bf16[48,1,2,1280]{3,2,1,0:T(2,128)(2,1)S(1)} %bitcast.84), channel_id=1, replica_groups=mesh['dp'=2,'expert'=8,'tensor'=2] {'tensor'}, dimensions={0}, use_global_device_ids=true | all-gather | bytes 737280 | tf_op jit(solution)/shard_map/all_gather | solution.py:80
  51.3 2.0 reshape.74
  53.3 11.1 %all_gather.12 = bf16[96,1,2,1280]{3,2,1,0:T(2,128)(2,1)} all-gather(bf16[48,1,2,1280]{3,2,1,0:T(2,128)(2,1)} %bitcast.4), channel_id=1, replica_groups=mesh['dp'=2,'expert'=8,'tensor'=2] {'tensor'}, dimensions={0}, use_global_device_ids=true | all-gather | bytes 737280 | tf_op jit(solution)/shard_map/all_gather | solution.py:105
  64.3 2.0 reshape.72
  66.3 2.7 multiply_convert_fusion
  69.0 3.5 %fusion.36 = bf16[192,1280]{1,0:T(8,128)(2,1)S(1)} fusion(f32[192,1280]{1,0:T(8,128)S(1)} %get-tuple-element.13, bf16[192,1280]{1,0:T(8,128)(2,1)} %reshape.72, bf16[1,1280,1280]{2,1,0:T(8,128)(2,1)} %param.11), kind=kOutput, calls=%fused_computation.48 | convolution fusion | flops 634060800 | bytes 5242880 | tf_op jit(solution)/shard_map/dot_general | solution.py:68
  73.3 2.2 fusion.16
  75.6 3.8 %fusion.20 = f32[192,1280]{1,0:T(8,128)} fusion(bf16[192,1280]{1,0:T(8,128)(2,1)} %get-tuple-element.12, bf16[1,1280,1280]{2,1,0:T(8,128)(2,1)} %param.11), kind=kOutput, calls=%fused_computation.24 | convolution fusion | flops 629145600 | bytes 4751360 | tf_op jit(solution)/shard_map/dot_general | solution.py:87
  79.4 2.1 all_to_all.90
  81.6 2.1 all_to_all.94
  83.7 1.9 copy.45
  85.6 4.2 %all-to-all-start.4 = ((bf16[192,2,640]{2,0,1:T(8,128)(2,1)}), bf16[192,2,640]{2,0,1:T(8,128)(2,1)}, u32[]{:S(2)}, u32[]{:S(2)}) async-start(bf16[192,2,640]{2,0,1:T(8,128)(2,1)} %copy.45), calls=%async_computation.6 | async-start | bytes 983040 | tf_op jit(solution)/shard_map/all_to_all | solution.py:122
  89.8 1.9 copy.46
  91.7 15.8 %all_gather.14 = bf16[384,1280]{1,0:T(8,128)(2,1)} all-gather(bf16[192,1280]{1,0:T(8,128)(2,1)} %copy-done.2), channel_id=1, replica_groups=mesh['dp'=2,'expert'=8,'tensor'=2] {'dp'}, dimensions={0}, use_global_device_ids=true | all-gather | bytes 1474560 | tf_op jit(solution)/shard_map/all_gather | solution.py:125
  107.5 4.2 %all-to-all-start.5 = ((bf16[192,2,640]{2,0,1:T(8,128)(2,1)}), bf16[192,2,640]{2,0,1:T(8,128)(2,1)}, u32[]{:S(2)}, u32[]{:S(2)}) async-start(bf16[192,2,640]{2,0,1:T(8,128)(2,1)} %copy.46), calls=%async_computation.7 | async-start | bytes 983040 | tf_op jit(solution)/shard_map/all_to_all | solution.py:123
  111.7 17.8 %all_gather.15 = bf16[384,1280]{1,0:T(8,128)(2,1)} all-gather(bf16[192,1280]{1,0:T(8,128)(2,1)} %get-tuple-element.12), channel_id=1, replica_groups=mesh['dp'=2,'expert'=8,'tensor'=2] {'dp'}, dimensions={0}, use_global_device_ids=true | all-gather | bytes 1474560 | tf_op jit(solution)/shard_map/all_gather | solution.py:126
  129.6 1.1 convert_element_type.53
  131.4 3.6 %all-to-all-start.2 = ((bf16[48,1,2,1280]{3,2,1,0:T(2,128)(2,1)}), bf16[48,1,2,1280]{3,2,1,0:T(2,128)(2,1)S(1)}, u32[]{:S(2)}, u32[]{:S(2)}) async-start(bf16[48,1,2,1280]{3,2,1,0:T(2,128)(2,1)} %bitcast.85), calls=%async_computation.3 | async-start | bytes 491520 | tf_op jit(solution)/shard_map/all_to_all | solution.py:113
  135.0 3.6 %fusion.24 = bf16[1,640,1280]{2,1,0:T(8,128)(2,1)} fusion(bf16[384,640]{1,0:T(8,128)(2,1)} %bitcast.20, bf16[384,1280]{1,0:T(8,128)(2,1)} %all_gather.14), kind=kOutput, calls=%fused_computation.30 | convolution fusion | flops 629964800 | bytes 3112960 | tf_op jit(solution)/shard_map/dot_general | solution.py:62
  138.6 3.6 %fusion.25 = bf16[1,1280,640]{2,1,0:T(8,128)(2,1)} fusion(bf16[384,1280]{1,0:T(8,128)(2,1)} %all_gather.15, bf16[384,640]{1,0:T(8,128)(2,1)} %bitcast.23), kind=kOutput, calls=%fused_computation.31 | convolution fusion | flops 629964800 | bytes 3112960 | tf_op jit(solution)/shard_map/dot_general | solution.py:62
  142.2 1.7 convert_element_type.55
  144.0 1.7 reshape.77
  145.7 5.1 %all-to-all-start.3 = ((bf16[48,1,2,1280]{3,2,1,0:T(2,128)(2,1)}), bf16[48,1,2,1280]{3,2,1,0:T(2,128)(2,1)}, u32[]{:S(2)}, u32[]{:S(2)}) async-start(bf16[48,1,2,1280]{3,2,1,0:T(2,128)(2,1)} %bitcast.86), calls=%async_computation.5 | async-start | bytes 491520 | tf_op jit(solution)/shard_map/all_to_all | solution.py:93
  151.7 1.0 reshape.76
  152.7 4.1 %multiply_reduce_fusion.2 = (f32[6,16]{1,0:T(8,128)S(1)}, f32[6,256,16]{1,2,0:T(8,128)}) fusion(f32[6,256,16]{1,2,0:T(8,128)} %get-tuple-element.9, f32[6,16]{1,0:T(8,128)S(1)} %get-tuple-element.8, bf16[6,16,1280]{2,1,0:T(8,128)(2,1)S(1)} %reshape.76, bf16[6,256,1280]{2,1,0:T(8,128)(2,1)} %param.6, f32[1280]{0:T(1024)} %param.8, ...), kind=kOutput, calls=%fused_computation.54 | convolution fusion | flops 72818592 | bytes 4392704 | tf_op jit(solution)/shard_map/bnd,bmd->bmn/dot_general | solution.py:34
  156.9 5.4 %fusion.43 = f32[6,256,1280]{2,1,0:T(8,128)} fusion(bf16[6,16,1280]{2,1,0:T(8,128)(2,1)S(1)} %reshape.76, f32[6,16]{1,0:T(8,128)S(1)} %get-tuple-element.8, f32[6,256,16]{1,2,0:T(8,128)} %copy-done.3), kind=kOutput, calls=%fused_computation.61 | convolution fusion | flops 62988640 | bytes 8208768 | tf_op jit(solution)/shard_map/bmn,bnd->bmd/dot_general | solution.py:37
  162.2 1.8 copy.49
  164.0 1.0 reshape.78
  165.1 3.3 multiply_reduce_fusion.1
  168.4 1.1 multiply_add_fusion
  169.5 4.5 %convolution_bitcast_fusion = f32[1280,16]{0,1:T(8,128)} fusion(f32[6,256,16]{1,2,0:T(8,128)S(1)} %multiply_add_fusion, bf16[6,256,1280]{2,1,0:T(8,128)(2,1)} %param.6, f32[1280]{0:T(1024)} %param.8, f32[6,256]{1,0:T(8,128)S(1)} %add_rsqrt_fusion, f32[6,256]{1,0:T(8,128)S(1)} %broadcast_multiply_fusion.2), kind=kOutput, calls=%fused_computation.34 | convolution fusion | flops 387317760 | bytes 4129792 | tf_op jit(solution)/shard_map/bmd,bmn->dn/dot_general | solution.py:50
  174.0 10.6 %fusion.14 = (f32[1280]{0:T(1024)S(1)}, f32[6,256]{1,0:T(8,128)S(1)}, f32[6,256]{1,0:T(8,128)S(1)}, f32[6,256,1280]{2,1,0:T(8,128)}) fusion(bf16[6,256,1280]{2,1,0:T(8,128)(2,1)} %param.6, f32[6,256]{1,0:T(8,128)S(1)} %add_rsqrt_fusion, f32[6,256]{1,0:T(8,128)S(1)} %broadcast_multiply_fusion.2, f32[1280]{0:T(1024)S(1)} %copy-done.7, ...), kind=kOutput, calls=%fused_computation.16 | convolution fusion | flops 397143808 | bytes 19834880 | tf_op jit(solution)/shard_map/bmn,dn->bmd/dot_general | solution.py:47
  184.7 86.7 %all-reduce.3.cloned.1.call-done = f32[1280,16]{0,1:T(8,128)} async-done(((f32[1280,16]{0,1:T(8,128)}), f32[1280,16]{0,1:T(8,128)}) %all-reduce.3.cloned.1.call-update) | async-done | bytes 81936 | tf_op jit(solution)/shard_map/psum | solution.py:11
  271.3 8.4 %fusion.13 = bf16[6,256,1280]{2,1,0:T(8,128)(2,1)} fusion(bf16[6,256,1280]{2,1,0:T(8,128)(2,1)} %param.6, bf16[6,256,1280]{2,1,0:T(8,128)(2,1)} %param.7, f32[6,256,1280]{2,1,0:T(8,128)} %get-tuple-element.18, f32[6,256]{1,0:T(8,128)S(1)} %get-tuple-element.19, f32[6,256]{1,0:T(8,128)S(1)} %get-tuple-element.20, f32[1280]{0:T(1024)S(1)} %copy-done.7, ...), kind=kLoop, calls=%fused_computation.15 | loop fusion | flops 21626880 | bytes 19690496 | tf_op jit(solution)/shard_map/convert_element_type | solution.py:119
  279.7 32.9 %psum.28 = f32[1280]{0:T(1024)S(1)} all-reduce(f32[1280]{0:T(1024)S(1)} %get-tuple-element.5), channel_id=1, replica_groups=mesh['dp'=2,'expert'=8,'tensor'=2] {'expert','tensor'}, use_global_device_ids=true, to_apply=%region_13.0 | all-reduce | flops 1280 | bytes 10240 | tf_op jit(solution)/shard_map/psum | solution.py:11
  312.6 5.6 %psum.29 = f32[1280]{0:T(1024)} all-reduce(f32[1280]{0:T(1024)S(1)} %psum.28), channel_id=1, replica_groups=mesh['dp'=2,'expert'=8,'tensor'=2] {'dp'}, use_global_device_ids=true, to_apply=%region_14.0 | all-reduce | flops 1280 | bytes 10240 | tf_op jit(solution)/shard_map/psum | solution.py:12
  318.2 1.5 copy.53
  (40 shorter events, 5.0 us)
Async XLA Ops:
  7.2 59.2 %copy-start = (bf16[1,1280,1280]{2,1,0:T(8,128)(2,1)S(1)}, bf16[1,1280,1280]{2,1,0:T(8,128)(2,1)}, u32[]{:S(2)}) copy-start(bf16[1,1280,1280]{2,1,0:T(8,128)(2,1)} %param.10) | copy-start | bytes 9830404
  7.2 6.3 %copy-start.1 = (bf16[6,256,1280]{2,1,0:T(8,128)(2,1)S(1)}, bf16[6,256,1280]{2,1,0:T(8,128)(2,1)}, u32[]{:S(2)}) copy-start(bf16[6,256,1280]{2,1,0:T(8,128)(2,1)} %param.6) | copy-start | bytes 11796484
  7.2 6.3 %copy-start.6 = (f32[1280]{0:T(1024)S(1)}, f32[1280]{0:T(1024)}, u32[]{:S(2)}) copy-start(f32[1280]{0:T(1024)} %param.8) | copy-start | bytes 15364
  7.2 6.3 %copy-start.4 = (bf16[1280,16]{0,1:T(8,128)(2,1)S(1)}, bf16[1280,16]{0,1:T(8,128)(2,1)}, u32[]{:S(2)}) copy-start(bf16[1280,16]{0,1:T(8,128)(2,1)} %param.9) | copy-start | bytes 122884
  15.1 0.8 copy-start.3
  22.0 15.7 %all-to-all-start.1 = ((bf16[6,8,2,1280]{3,2,0,1:T(2,128)(2,1)}), bf16[6,8,2,1280]{3,2,0,1:T(2,128)(2,1)S(1)}, u32[]{:S(2)}, u32[]{:S(2)}) async-start(bf16[6,8,2,1280]{3,2,0,1:T(2,128)(2,1)} %copy.39), calls=%async_computation.1 | async-start | bytes 491520 | tf_op jit(solution)/shard_map/all_to_all | solution.py:79
  37.7 15.6 %all-to-all-start = ((bf16[6,8,2,1280]{3,2,0,1:T(2,128)(2,1)}), bf16[6,8,2,1280]{3,2,0,1:T(2,128)(2,1)}, u32[]{:S(2)}, u32[]{:S(2)}) async-start(bf16[6,8,2,1280]{3,2,0,1:T(2,128)(2,1)} %copy.37), calls=%async_computation | async-start | bytes 491520 | tf_op jit(solution)/shard_map/all_to_all | solution.py:104
  42.2 87.4 %reduce-scatter.3.cloned.1.call-start = ((), (), s32[]{:S(2)}) async-start(), calls=%async_computation.8 | async-start | bytes 1474560 | tf_op jit(solution)/shard_map/reduce_scatter | solution.py:109
  72.5 0.8 copy-start.2
  75.5 66.7 %reduce-scatter.5.cloned.1.call-start = ((), (), s32[]{:S(2)}) async-start(), calls=%async_computation.9 | async-start | bytes 1474560 | tf_op jit(solution)/shard_map/reduce_scatter | solution.py:86
  85.6 22.0 %all-to-all-start.4 = ((bf16[192,2,640]{2,0,1:T(8,128)(2,1)}), bf16[192,2,640]{2,0,1:T(8,128)(2,1)}, u32[]{:S(2)}, u32[]{:S(2)}) async-start(bf16[192,2,640]{2,0,1:T(8,128)(2,1)} %copy.45), calls=%async_computation.6 | async-start | bytes 983040 | tf_op jit(solution)/shard_map/all_to_all | solution.py:122
  107.5 23.9 %all-to-all-start.5 = ((bf16[192,2,640]{2,0,1:T(8,128)(2,1)}), bf16[192,2,640]{2,0,1:T(8,128)(2,1)}, u32[]{:S(2)}, u32[]{:S(2)}) async-start(bf16[192,2,640]{2,0,1:T(8,128)(2,1)} %copy.46), calls=%async_computation.7 | async-start | bytes 983040 | tf_op jit(solution)/shard_map/all_to_all | solution.py:123
  131.4 14.3 %all-to-all-start.2 = ((bf16[48,1,2,1280]{3,2,1,0:T(2,128)(2,1)}), bf16[48,1,2,1280]{3,2,1,0:T(2,128)(2,1)S(1)}, u32[]{:S(2)}, u32[]{:S(2)}) async-start(bf16[48,1,2,1280]{3,2,1,0:T(2,128)(2,1)} %bitcast.85), calls=%async_computation.3 | async-start | bytes 491520 | tf_op jit(solution)/shard_map/all_to_all | solution.py:113
  145.7 16.5 %all-to-all-start.3 = ((bf16[48,1,2,1280]{3,2,1,0:T(2,128)(2,1)}), bf16[48,1,2,1280]{3,2,1,0:T(2,128)(2,1)}, u32[]{:S(2)}, u32[]{:S(2)}) async-start(bf16[48,1,2,1280]{3,2,1,0:T(2,128)(2,1)} %bitcast.86), calls=%async_computation.5 | async-start | bytes 491520 | tf_op jit(solution)/shard_map/all_to_all | solution.py:93
  150.8 120.5 %all-reduce.3.cloned.1.call-start = ((), (), s32[]{:S(2)}) async-start(), calls=%async_computation.10 | async-start | bytes 163840 | tf_op jit(solution)/shard_map/psum | solution.py:11
  168.3 5.6 %copy-start.5 = (bf16[1280,16]{0,1:T(8,128)(2,1)S(1)}, bf16[1280,16]{0,1:T(8,128)(2,1)}, u32[]{:S(2)}) copy-start(bf16[1280,16]{0,1:T(8,128)(2,1)} %param.9) | copy-start | bytes 122884
  168.3 5.6 %copy-start.7 = (f32[1280]{0:T(1024)S(1)}, f32[1280]{0:T(1024)}, u32[]{:S(2)}) copy-start(f32[1280]{0:T(1024)} %param.8) | copy-start | bytes 15364
  184.6 133.6 %all-reduce.5.cloned.1.call-start = ((), (), s32[]{:S(2)}) async-start(), calls=%async_computation.11 | async-start | bytes 163840 | tf_op jit(solution)/shard_map/psum | solution.py:12
Sparse Core Ops, SparseCore 0:
  75.6 19.4 reduce-scatter.2
  98.0 19.6 reduce-scatter.4
  184.7 86.5 all-reduce.2
  273.4 21.9 all-reduce.4
